TPU v7x, 32 devices: a whole 2x2x4 slice. The times are simulated.
32 devices in a mesh: dp: 8 (over y, x, core), seq: 4 (over z).
Axes of the slice: x: 2, y: 2, z: 4, core: 2. Of those that a mesh axis runs over, the one named last changes fastest.
Arguments:
- queries: bfloat16 [8192, 1664], P(('dp', 'seq')), parts along dimension 0, may hold values from -6 to 6
- key_rows: bfloat16 [8192, 1664], P(('dp', 'seq')), parts along dimension 0, may hold values from -6 to 6
- value_rows: bfloat16 [8192, 1664], P(('dp', 'seq')), parts along dimension 0, may hold values from -6 to 6
Outputs:
- merged_tokens: bfloat16 [2048, 6656], P('dp', 'seq'), parts along dimension 0
There are 8 independent parts, one for each index of `dp`. A program takes and returns all parts, laid end to end along the dimension named above; each array names one. Nothing has to cross between parts.
All inputs are finite; a program needn't handle non-finite values.
Results may differ from a plain program's by a relative error of at most 0.005.
Values may be sent and summed in bfloat16 or wider, within the bound.
A program may use at most 128 MiB of HBM per device.

v0:
```python
import functools
import math

import jax
import jax.numpy as jnp
from jax import lax
from jax.experimental import pallas as pl
from jax.experimental.pallas import tpu as pltpu
from jax.sharding import PartitionSpec as P

HEAD_DIM = 128
GRID_W = 64
MERGE = 2


def by_heads(queries, key_rows, value_rows, score_scale):
    tok_rows, width = queries.shape
    heads = width // HEAD_DIM
    groups = lax.axis_size("seq")
    padded_heads = -(-heads // groups) * groups

    def spread(source):
        shaped = source.reshape(tok_rows, heads, HEAD_DIM)
        shaped = jnp.pad(shaped, ((0, 0), (0, padded_heads - heads), (0, 0)))
        return shaped.reshape(tok_rows, groups, padded_heads // groups, HEAD_DIM)

    head_query = lax.all_to_all(spread(queries), "seq", split_axis=1, concat_axis=0, tiled=True)
    head_key = lax.all_to_all(spread(key_rows), "seq", split_axis=1, concat_axis=0, tiled=True)
    head_value = lax.all_to_all(spread(value_rows), "seq", split_axis=1, concat_axis=0, tiled=True)
    total_rows = head_query.shape[0]
    head_count = head_query.shape[2]
    flat_key = head_key.reshape(total_rows, head_count, HEAD_DIM)
    flat_value = head_value.reshape(total_rows, head_count, HEAD_DIM)
    step_rows = math.gcd(total_rows, 512)
    blocks = head_query.reshape(total_rows // step_rows, step_rows, head_count, HEAD_DIM)

    def one_block(query_block):
        scores = (
            jnp.einsum("qhd,khd->hqk", query_block, flat_key, preferred_element_type=jnp.float32)
            * score_scale
        )
        row_max = jnp.max(scores, axis=-1, keepdims=True)
        weights = jnp.exp(scores - row_max)
        totals = jnp.sum(weights, axis=-1, keepdims=True)
        weighted = jnp.einsum(
            "hqk,khd->qhd",
            weights.astype(jnp.bfloat16),
            flat_value,
            preferred_element_type=jnp.float32,
        )
        return (weighted / totals.transpose(1, 0, 2)).astype(jnp.bfloat16)

    result = lax.map(one_block, blocks).reshape(total_rows, 1, head_count, HEAD_DIM)
    result = lax.all_to_all(result, "seq", split_axis=0, concat_axis=1, tiled=True)
    return result.reshape(tok_rows, padded_heads, HEAD_DIM)[:, :heads].reshape(tok_rows, width)


def split_features(queries, key_rows, value_rows):
    score_scale = 1.0 / math.sqrt(HEAD_DIM)
    attended = by_heads(queries, key_rows, value_rows, score_scale)
    tok_rows, width = attended.shape
    grid_rows = tok_rows // GRID_W
    shuffled = attended.reshape(grid_rows // 2, 2, GRID_W // 2, 2, width).transpose(0, 2, 1, 3, 4)
    shuffled = shuffled.reshape(grid_rows // 2 * (GRID_W // 2), 4 * width)
    return lax.all_to_all(shuffled, "seq", split_axis=1, concat_axis=0, tiled=True)


def head_kernel(
    n, heads, query_rows,
    q_ref, k_ref, v_ref, out_ref,
    qbuf, kbuf, vbuf, obuf, osend,
    in_send, in_recv, out_send, out_recv, ready, far, everyone,
):
    me = lax.axis_index("seq")
    flip = lax.rem(lax.axis_index("dp"), 2)
    base, extra = heads // n, heads % n
    lead = 1 if extra else 0
    slots = base + lead
    rows = q_ref.shape[0]
    total_rows = rows * n
    score_scale = 1.0 / math.sqrt(HEAD_DIM)

    def place(device):
        return flip * (n - 1 - device) + (1 - flip) * device

    def head_of(device, slot):
        at = place(device)
        regular = at * base + slot - lead
        if not lead:
            return regular
        return jnp.where(slot == 0, n * base + at, regular)

    def has(device, slot):
        if not lead:
            return slot >= 0
        return jnp.logical_or(slot > 0, place(device) < extra)

    def columns(head):
        return pl.ds(pl.multiple_of(head * HEAD_DIM, HEAD_DIM), HEAD_DIM)

    def rows_of(device):
        return pl.ds(pl.multiple_of(device * rows, rows), rows)

    peers = (n - 1 - me, lax.rem(me + n // 2, n), me + 1 - 2 * lax.rem(me, 2))
    tensors = ((k_ref, kbuf), (q_ref, qbuf), (v_ref, vbuf))

    def inward(t, slot, peer, source, owner):
        ref, buf = tensors[t]
        return pltpu.make_async_remote_copy(
            src_ref=ref.at[:, columns(head_of(owner, slot))],
            dst_ref=buf.at[slot, rows_of(source), :],
            send_sem=in_send.at[t, slot, peer],
            recv_sem=in_recv.at[t, slot, source],
            device_id={"seq": peer},
            device_id_type=pl.DeviceIdType.MESH,
        )

    def inward_own(t, slot):
        ref, buf = tensors[t]
        return pltpu.make_async_copy(
            ref.at[:, columns(head_of(me, slot))],
            buf.at[slot, rows_of(me), :],
            in_recv.at[t, slot, me],
        )

    def outward(slot, peer, source):
        return pltpu.make_async_remote_copy(
            src_ref=osend.at[slot, peer],
            dst_ref=out_ref.at[:, columns(head_of(source, slot))],
            send_sem=out_send.at[slot, peer],
            recv_sem=out_recv.at[slot, source],
            device_id={"seq": peer},
            device_id_type=pl.DeviceIdType.MESH,
        )

    def outward_own(slot):
        return pltpu.make_async_copy(
            osend.at[slot, me],
            out_ref.at[:, columns(head_of(me, slot))],
            out_recv.at[slot, me],
        )

    partner, mate = peers[0], peers[2]
    inner = (me > 0) & (me < n - 1)
    early = lead + 1

    def tell(sem, device):
        pl.semaphore_signal(
            sem, inc=1, device_id={"seq": device}, device_id_type=pl.DeviceIdType.MESH
        )

    barrier = pltpu.get_barrier_semaphore()

    @pl.when(inner)
    def _():
        tell(barrier, partner)
        tell(barrier, mate)

    pl.semaphore_wait(barrier, 1)

    @pl.when(inner)
    def _():
        for slot in range(early):
            for t in range(3):
                @pl.when(has(partner, slot))
                def _():
                    inward(t, slot, partner, me, partner).start()
        pl.semaphore_wait(ready, 1)
        tell(far, partner)
        pl.semaphore_wait(far, 1)
        tell(everyone, mate)

    @pl.when(jnp.logical_not(inner))
    def _():
        tell(ready, mate)
        pl.semaphore_wait(everyone, 1)

    @pl.loop(0, slots)
    def _(slot):
        for t in range(3):
            for peer in peers:
                fresh = has(peer, slot)
                if peer is partner:
                    fresh = fresh & ((slot >= early) | jnp.logical_not(inner))

                @pl.when(fresh)
                def _():
                    inward(t, slot, peer, me, peer).start()

            @pl.when(has(me, slot))
            def _():
                inward_own(t, slot).start()

    @pl.loop(0, slots)
    def _(slot):
        @pl.when(has(me, slot))
        def _():
            for t in range(3):
                for peer in peers:
                    inward(t, slot, peer, peer, me).wait_recv()
                inward_own(t, slot).wait()

            @pl.loop(0, total_rows // query_rows)
            def _(block):
                at = pl.ds(pl.multiple_of(block * query_rows, query_rows), query_rows)
                scores = lax.dot_general(
                    qbuf[slot, at, :], kbuf[slot], (((1,), (1,)), ((), ())),
                    preferred_element_type=jnp.float32,
                ) * score_scale
                row_max = jnp.max(scores, axis=-1, keepdims=True)
                weights = jnp.exp(scores - row_max)
                totals = jnp.sum(weights, axis=-1, keepdims=True)
                weighted = jnp.dot(
                    weights.astype(jnp.bfloat16), vbuf[slot], preferred_element_type=jnp.float32
                )
                obuf[at, :] = weighted / totals

            half = GRID_W // MERGE
            for a in range(MERGE):
                for b in range(MERGE):
                    for i in range(total_rows // GRID_W // MERGE):
                        part = obuf[pl.ds((MERGE * i + a) * GRID_W + b, half, stride=MERGE), :]
                        osend[slot, MERGE * a + b, i * half:(i + 1) * half, :] = part.astype(jnp.bfloat16)
            for peer in reversed(peers):
                outward(slot, peer, me).start()
            outward_own(slot).start()

    @pl.loop(0, slots)
    def _(slot):
        for peer in peers:
            @pl.when(has(peer, slot))
            def _():
                for t in range(3):
                    inward(t, slot, peer, me, peer).wait_send()
                outward(slot, peer, peer).wait_recv()

        @pl.when(has(me, slot))
        def _():
            for peer in peers:
                outward(slot, peer, me).wait_send()
            outward_own(slot).wait()


def on_device(queries, key_rows, value_rows):
    n = lax.axis_size("seq")
    if n != MERGE * MERGE:
        return split_features(queries, key_rows, value_rows)
    rows, width = queries.shape
    heads = width // HEAD_DIM
    slots = -(-heads // n)
    total_rows = rows * n
    merged_rows = total_rows // (MERGE * MERGE)
    anywhere = pl.BlockSpec(memory_space=pl.ANY)
    gathered = pltpu.VMEM((slots, total_rows, HEAD_DIM), jnp.bfloat16)
    return pl.pallas_call(
        functools.partial(head_kernel, n, heads, math.gcd(total_rows, 256)),
        out_shape=pltpu.VMEM((merged_rows, width), jnp.bfloat16),
        in_specs=[anywhere] * 3,
        out_specs=pl.BlockSpec(memory_space=pltpu.VMEM),
        scratch_shapes=[
            gathered,
            gathered,
            gathered,
            pltpu.VMEM((total_rows + 8, HEAD_DIM), jnp.float32),
            pltpu.VMEM((slots, n, merged_rows, HEAD_DIM), jnp.bfloat16),
            pltpu.SemaphoreType.DMA((3, slots, n)),
            pltpu.SemaphoreType.DMA((3, slots, n)),
            pltpu.SemaphoreType.DMA((slots, n)),
            pltpu.SemaphoreType.DMA((slots, n)),
            pltpu.SemaphoreType.REGULAR,
            pltpu.SemaphoreType.REGULAR,
            pltpu.SemaphoreType.REGULAR,
        ],
        compiler_params=pltpu.CompilerParams(collective_id=0, has_side_effects=True),
        name="heads_exchange",
    )(queries, key_rows, value_rows)


def solution(mesh):
    placed = (P(("dp", "seq"), None), P(("dp", "seq"), None), P(("dp", "seq"), None))
    return jax.shard_map(
        on_device, mesh=mesh, in_specs=placed, out_specs=P("dp", "seq"), check_vma=False
    )
```

profile of v0, /device:TPU:1, one launch (start us, length us, event | category | flops | bytes accessed | tf_op | source)
XLA Modules:
  0.0 79.1 jit_solution(11183016790867309534)
XLA Ops:
  0.0 78.2 %heads_exchange.1 = bf16[256,1664]{1,0:T(8,128)(2,1)S(1)} custom-call(bf16[256,1664]{1,0:T(8,128)(2,1)} %q_ref.1, bf16[256,1664]{1,0:T(8,128)(2,1)} %k_ref.1, bf16[256,1664]{1,0:T(8,128)(2,1)} %v_ref.1), custom_call_target="tpu_custom_call" | custom-call | tf_op jit(solution)/shard_map/heads_exchange/pallas_call | solution.py:255
  78.2 0.9 %copy.5 = bf16[256,1664]{1,0:T(8,128)(2,1)} copy(bf16[256,1664]{1,0:T(8,128)(2,1)S(1)} %heads_exchange.1) | data formatting | bytes 1703936
where the time goes:
time: 79.2 us; the launch traced here: 79.1 us
  Pallas kernels  78.2 us (99%)
  local copies, waits for them, and re-layouts  0.9 us (1%)
    pallas_call x1, Pallas kernels, on_device(): pl.pallas_call(functools.partial(head_kernel, n, heads, math.gcd(total_ro...  78.2 us

commit v1 on v0

--- a/solution.py
+++ b/solution.py
@@ -68,8 +68,8 @@
 def head_kernel(
     n, heads, query_rows,
     q_ref, k_ref, v_ref, out_ref,
-    qbuf, kbuf, vbuf, obuf, osend,
-    in_send, in_recv, out_send, out_recv, ready, far, everyone,
+    held, obuf, osend,
+    landed, sent, merged, ready, far, everyone,
 ):
     me = lax.axis_index("seq")
     flip = lax.rem(lax.axis_index("dp"), 2)
@@ -98,47 +98,46 @@
     def columns(head):
         return pl.ds(pl.multiple_of(head * HEAD_DIM, HEAD_DIM), HEAD_DIM)
 
-    def rows_of(device):
-        return pl.ds(pl.multiple_of(device * rows, rows), rows)
+    def rows_of(tensor, device):
+        return pl.ds(pl.multiple_of(tensor * total_rows + device * rows, rows), rows)
 
     peers = (n - 1 - me, lax.rem(me + n // 2, n), me + 1 - 2 * lax.rem(me, 2))
-    tensors = ((k_ref, kbuf), (q_ref, qbuf), (v_ref, vbuf))
-
-    def inward(t, slot, peer, source, owner):
-        ref, buf = tensors[t]
+    tensors = (k_ref, q_ref, v_ref)
+
+    def inward(t, slot, peer):
         return pltpu.make_async_remote_copy(
-            src_ref=ref.at[:, columns(head_of(owner, slot))],
-            dst_ref=buf.at[slot, rows_of(source), :],
-            send_sem=in_send.at[t, slot, peer],
-            recv_sem=in_recv.at[t, slot, source],
+            src_ref=tensors[t].at[:, columns(head_of(peer, slot))],
+            dst_ref=held.at[slot, rows_of(t, me), :],
+            send_sem=sent,
+            recv_sem=landed.at[slot],
             device_id={"seq": peer},
             device_id_type=pl.DeviceIdType.MESH,
         )
 
     def inward_own(t, slot):
-        ref, buf = tensors[t]
         return pltpu.make_async_copy(
-            ref.at[:, columns(head_of(me, slot))],
-            buf.at[slot, rows_of(me), :],
-            in_recv.at[t, slot, me],
-        )
-
-    def outward(slot, peer, source):
+            tensors[t].at[:, columns(head_of(me, slot))],
+            held.at[slot, rows_of(t, me), :],
+            landed.at[slot],
+        )
+
+    def outward(slot, peer):
         return pltpu.make_async_remote_copy(
             src_ref=osend.at[slot, peer],
-            dst_ref=out_ref.at[:, columns(head_of(source, slot))],
-            send_sem=out_send.at[slot, peer],
-            recv_sem=out_recv.at[slot, source],
+            dst_ref=out_ref.at[:, columns(head_of(me, slot))],
+            send_sem=sent,
+            recv_sem=merged,
             device_id={"seq": peer},
             device_id_type=pl.DeviceIdType.MESH,
         )
 
     def outward_own(slot):
         return pltpu.make_async_copy(
-            osend.at[slot, me],
-            out_ref.at[:, columns(head_of(me, slot))],
-            out_recv.at[slot, me],
-        )
+            osend.at[slot, me], out_ref.at[:, columns(head_of(me, slot))], merged
+        )
+
+    def wait_bytes(ref, sem):
+        pltpu.make_async_copy(ref, ref, sem).wait()
 
     partner, mate = peers[0], peers[2]
     inner = (me > 0) & (me < n - 1)
@@ -164,7 +163,7 @@
             for t in range(3):
                 @pl.when(has(partner, slot))
                 def _():
-                    inward(t, slot, partner, me, partner).start()
+                    inward(t, slot, partner).start()
         pl.semaphore_wait(ready, 1)
         tell(far, partner)
         pl.semaphore_wait(far, 1)
@@ -185,7 +184,7 @@
 
                 @pl.when(fresh)
                 def _():
-                    inward(t, slot, peer, me, peer).start()
+                    inward(t, slot, peer).start()
 
             @pl.when(has(me, slot))
             def _():
@@ -195,23 +194,22 @@
     def _(slot):
         @pl.when(has(me, slot))
         def _():
-            for t in range(3):
-                for peer in peers:
-                    inward(t, slot, peer, peer, me).wait_recv()
-                inward_own(t, slot).wait()
+            wait_bytes(held.at[slot], landed.at[slot])
 
             @pl.loop(0, total_rows // query_rows)
             def _(block):
                 at = pl.ds(pl.multiple_of(block * query_rows, query_rows), query_rows)
+                from_q = pl.ds(pl.multiple_of(total_rows + block * query_rows, query_rows), query_rows)
                 scores = lax.dot_general(
-                    qbuf[slot, at, :], kbuf[slot], (((1,), (1,)), ((), ())),
+                    held[slot, from_q, :], held[slot, pl.ds(0, total_rows), :], (((1,), (1,)), ((), ())),
                     preferred_element_type=jnp.float32,
                 ) * score_scale
                 row_max = jnp.max(scores, axis=-1, keepdims=True)
                 weights = jnp.exp(scores - row_max)
                 totals = jnp.sum(weights, axis=-1, keepdims=True)
                 weighted = jnp.dot(
-                    weights.astype(jnp.bfloat16), vbuf[slot], preferred_element_type=jnp.float32
+                    weights.astype(jnp.bfloat16), held[slot, pl.ds(2 * total_rows, total_rows), :],
+                    preferred_element_type=jnp.float32,
                 )
                 obuf[at, :] = weighted / totals
 
@@ -222,23 +220,12 @@
                         part = obuf[pl.ds((MERGE * i + a) * GRID_W + b, half, stride=MERGE), :]
                         osend[slot, MERGE * a + b, i * half:(i + 1) * half, :] = part.astype(jnp.bfloat16)
             for peer in reversed(peers):
-                outward(slot, peer, me).start()
+                outward(slot, peer).start()
             outward_own(slot).start()
 
-    @pl.loop(0, slots)
-    def _(slot):
-        for peer in peers:
-            @pl.when(has(peer, slot))
-            def _():
-                for t in range(3):
-                    inward(t, slot, peer, me, peer).wait_send()
-                outward(slot, peer, peer).wait_recv()
-
-        @pl.when(has(me, slot))
-        def _():
-            for peer in peers:
-                outward(slot, peer, me).wait_send()
-            outward_own(slot).wait()
+    wait_bytes(out_ref, merged)
+    for _ in range(3):
+        wait_bytes(q_ref, sent)
 
 
 def on_device(queries, key_rows, value_rows):
@@ -251,22 +238,18 @@
     total_rows = rows * n
     merged_rows = total_rows // (MERGE * MERGE)
     anywhere = pl.BlockSpec(memory_space=pl.ANY)
-    gathered = pltpu.VMEM((slots, total_rows, HEAD_DIM), jnp.bfloat16)
     return pl.pallas_call(
         functools.partial(head_kernel, n, heads, math.gcd(total_rows, 256)),
         out_shape=pltpu.VMEM((merged_rows, width), jnp.bfloat16),
         in_specs=[anywhere] * 3,
         out_specs=pl.BlockSpec(memory_space=pltpu.VMEM),
         scratch_shapes=[
-            gathered,
-            gathered,
-            gathered,
+            pltpu.VMEM((slots, 3 * total_rows, HEAD_DIM), jnp.bfloat16),
             pltpu.VMEM((total_rows + 8, HEAD_DIM), jnp.float32),
             pltpu.VMEM((slots, n, merged_rows, HEAD_DIM), jnp.bfloat16),
-            pltpu.SemaphoreType.DMA((3, slots, n)),
-            pltpu.SemaphoreType.DMA((3, slots, n)),
-            pltpu.SemaphoreType.DMA((slots, n)),
-            pltpu.SemaphoreType.DMA((slots, n)),
+            pltpu.SemaphoreType.DMA((slots,)),
+            pltpu.SemaphoreType.DMA,
+            pltpu.SemaphoreType.DMA,
             pltpu.SemaphoreType.REGULAR,
             pltpu.SemaphoreType.REGULAR,
             pltpu.SemaphoreType.REGULAR,

time: 79.2 us -> 78.1 us (0.986)
  Pallas kernels: 78.2 us -> 77.1 us
    pallas_call x1, Pallas kernels: 78.2 us -> 77.1 us  [on_device(): pl.pallas_call(functools.partial(head_kernel, n, heads, math.gcd(total_ro...]
where the time goes in v1:
time: 78.1 us; the launch traced here: 78 us
  Pallas kernels  77.1 us (99%)
  local copies, waits for them, and re-layouts  0.9 us (1%)
    pallas_call x1, Pallas kernels, on_device(): pl.pallas_call(functools.partial(head_kernel, n, heads, math.gcd(total_ro...  77.1 us

profile of v1, /device:TPU:1, one launch (start us, length us, event | category | flops | bytes accessed | tf_op | source)
XLA Modules:
  0.0 78.0 jit_solution(4910037567078828246)
XLA Ops:
  0.0 77.1 %heads_exchange.1 = bf16[256,1664]{1,0:T(8,128)(2,1)S(1)} custom-call(bf16[256,1664]{1,0:T(8,128)(2,1)} %q_ref.1, bf16[256,1664]{1,0:T(8,128)(2,1)} %k_ref.1, bf16[256,1664]{1,0:T(8,128)(2,1)} %v_ref.1), custom_call_target="tpu_custom_call" | custom-call | tf_op jit(solution)/shard_map/heads_exchange/pallas_call | solution.py:241
  77.1 0.9 %copy.5 = bf16[256,1664]{1,0:T(8,128)(2,1)} copy(bf16[256,1664]{1,0:T(8,128)(2,1)S(1)} %heads_exchange.1) | data formatting | bytes 1703936

commit v2 on v1

--- a/solution.py
+++ b/solution.py
@@ -81,7 +81,8 @@
     score_scale = 1.0 / math.sqrt(HEAD_DIM)
 
     def place(device):
-        return flip * (n - 1 - device) + (1 - flip) * device
+        at = device + 1 - 2 * lax.rem(device, 2)
+        return flip * (n - 1 - at) + (1 - flip) * at
 
     def head_of(device, slot):
         at = place(device)
@@ -139,7 +140,9 @@
     def wait_bytes(ref, sem):
         pltpu.make_async_copy(ref, ref, sem).wait()
 
-    partner, mate = peers[0], peers[2]
+    partner, across, mate = peers
+    far_low = jnp.where(me < n // 2, n // 2, 0)
+    far_high = far_low + 1
     inner = (me > 0) & (me < n - 1)
     early = lead + 1
 
@@ -219,9 +222,35 @@
                     for i in range(total_rows // GRID_W // MERGE):
                         part = obuf[pl.ds((MERGE * i + a) * GRID_W + b, half, stride=MERGE), :]
                         osend[slot, MERGE * a + b, i * half:(i + 1) * half, :] = part.astype(jnp.bfloat16)
-            for peer in reversed(peers):
-                outward(slot, peer).start()
+            outward(slot, mate).start()
+
+            @pl.when(inner)
+            def _():
+                outward(slot, far_low).start()
+
+            @pl.when(jnp.logical_not(inner))
+            def _():
+                outward(slot, far_low).start()
+
             outward_own(slot).start()
+
+    @pl.when(inner)
+    def _():
+        for peer in (far_high,):
+            @pl.loop(0, slots)
+            def _(slot):
+                @pl.when(has(me, slot))
+                def _():
+                    outward(slot, peer).start()
+
+    @pl.when(jnp.logical_not(inner))
+    def _():
+        for peer in (far_high,):
+            @pl.loop(0, slots)
+            def _(slot):
+                @pl.when(has(me, slot))
+                def _():
+                    outward(slot, peer).start()
 
     wait_bytes(out_ref, merged)
     for _ in range(3):

time: 78.1 us -> 76.8 us (0.983)
  the two profiles are of different devices: /device:TPU:1 before, /device:TPU:9 now
where the time goes in v2:
time: 76.8 us; the launch traced here: 76.7 us
  Pallas kernels  75.8 us (99%)
  local copies, waits for them, and re-layouts  0.9 us (1%)
    pallas_call x1, Pallas kernels, on_device(): pl.pallas_call(functools.partial(head_kernel, n, heads, math.gcd(total_ro...  75.8 us

profile of v2, /device:TPU:9, one launch (start us, length us, event | category | flops | bytes accessed | tf_op | source)
XLA Modules:
  0.0 76.7 jit_solution(17861407251522159592)
XLA Ops:
  0.0 75.8 %heads_exchange.1 = bf16[256,1664]{1,0:T(8,128)(2,1)S(1)} custom-call(bf16[256,1664]{1,0:T(8,128)(2,1)} %q_ref.1, bf16[256,1664]{1,0:T(8,128)(2,1)} %k_ref.1, bf16[256,1664]{1,0:T(8,128)(2,1)} %v_ref.1), custom_call_target="tpu_custom_call" | custom-call | tf_op jit(solution)/shard_map/heads_exchange/pallas_call | solution.py:270
  75.8 0.9 %copy.5 = bf16[256,1664]{1,0:T(8,128)(2,1)} copy(bf16[256,1664]{1,0:T(8,128)(2,1)S(1)} %heads_exchange.1) | data formatting | bytes 1703936

commit v3 on v2

--- a/solution.py
+++ b/solution.py
@@ -68,8 +68,8 @@
 def head_kernel(
     n, heads, query_rows,
     q_ref, k_ref, v_ref, out_ref,
-    held, obuf, osend,
-    landed, sent, merged, ready, far, everyone,
+    held, obuf, osend, staged,
+    loaded, landed, sent, merged, ready, far,
 ):
     me = lax.axis_index("seq")
     flip = lax.rem(lax.axis_index("dp"), 2)
@@ -105,9 +105,9 @@
     peers = (n - 1 - me, lax.rem(me + n // 2, n), me + 1 - 2 * lax.rem(me, 2))
     tensors = (k_ref, q_ref, v_ref)
 
-    def inward(t, slot, peer):
+    def inward(t, slot, peer, source=None):
         return pltpu.make_async_remote_copy(
-            src_ref=tensors[t].at[:, columns(head_of(peer, slot))],
+            src_ref=tensors[t].at[:, columns(head_of(peer, slot))] if source is None else source,
             dst_ref=held.at[slot, rows_of(t, me), :],
             send_sem=sent,
             recv_sem=landed.at[slot],
@@ -158,11 +158,31 @@
         tell(barrier, partner)
         tell(barrier, mate)
 
+    left = me == n // 2 - 1
+
+    @pl.when(left)
+    def _():
+        for t in range(3):
+            pltpu.make_async_copy(
+                tensors[t].at[:, columns(head_of(partner, lead))], staged.at[t], loaded
+            ).start()
+
     pl.semaphore_wait(barrier, 1)
 
     @pl.when(inner)
     def _():
-        for slot in range(early):
+        @pl.when(left)
+        def _():
+            wait_bytes(staged, loaded)
+            for t in range(3):
+                inward(t, lead, partner, staged.at[t]).start()
+
+        @pl.when(jnp.logical_not(left))
+        def _():
+            for t in range(3):
+                inward(t, lead, partner).start()
+
+        for slot in range(lead):
             for t in range(3):
                 @pl.when(has(partner, slot))
                 def _():
@@ -170,12 +190,12 @@
         pl.semaphore_wait(ready, 1)
         tell(far, partner)
         pl.semaphore_wait(far, 1)
-        tell(everyone, mate)
+        tell(far, mate)
 
     @pl.when(jnp.logical_not(inner))
     def _():
         tell(ready, mate)
-        pl.semaphore_wait(everyone, 1)
+        pl.semaphore_wait(far, 1)
 
     @pl.loop(0, slots)
     def _(slot):
@@ -276,10 +296,11 @@
             pltpu.VMEM((slots, 3 * total_rows, HEAD_DIM), jnp.bfloat16),
             pltpu.VMEM((total_rows + 8, HEAD_DIM), jnp.float32),
             pltpu.VMEM((slots, n, merged_rows, HEAD_DIM), jnp.bfloat16),
+            pltpu.VMEM((3, rows, HEAD_DIM), jnp.bfloat16),
+            pltpu.SemaphoreType.DMA,
             pltpu.SemaphoreType.DMA((slots,)),
             pltpu.SemaphoreType.DMA,
             pltpu.SemaphoreType.DMA,
-            pltpu.SemaphoreType.REGULAR,
             pltpu.SemaphoreType.REGULAR,
             pltpu.SemaphoreType.REGULAR,
         ],

time: 76.8 us -> 76.9 us (level)
  no operation moved by 1% of the time
where the time goes in v3:
time: 76.9 us; the launch traced here: 76.7 us
  Pallas kernels  75.8 us (99%)
  local copies, waits for them, and re-layouts  0.9 us (1%)
    pallas_call x1, Pallas kernels, on_device(): pl.pallas_call(functools.partial(head_kernel, n, heads, math.gcd(total_ro...  75.8 us

profile of v3, /device:TPU:9, one launch (start us, length us, event | category | flops | bytes accessed | tf_op | source)
XLA Modules:
  0.0 76.7 jit_solution(642778425282600100)
XLA Ops:
  0.0 75.8 %heads_exchange.1 = bf16[256,1664]{1,0:T(8,128)(2,1)S(1)} custom-call(bf16[256,1664]{1,0:T(8,128)(2,1)} %q_ref.1, bf16[256,1664]{1,0:T(8,128)(2,1)} %k_ref.1, bf16[256,1664]{1,0:T(8,128)(2,1)} %v_ref.1), custom_call_target="tpu_custom_call" | custom-call | tf_op jit(solution)/shard_map/heads_exchange/pallas_call | solution.py:290
  75.8 0.9 %copy.5 = bf16[256,1664]{1,0:T(8,128)(2,1)} copy(bf16[256,1664]{1,0:T(8,128)(2,1)S(1)} %heads_exchange.1) | data formatting | bytes 1703936

commit v4 on v3

--- a/solution.py
+++ b/solution.py
@@ -105,12 +105,15 @@
     peers = (n - 1 - me, lax.rem(me + n // 2, n), me + 1 - 2 * lax.rem(me, 2))
     tensors = (k_ref, q_ref, v_ref)
 
+    def group_of(slot):
+        return slot - jnp.where(slot >= lead, lead, 0)
+
     def inward(t, slot, peer, source=None):
         return pltpu.make_async_remote_copy(
             src_ref=tensors[t].at[:, columns(head_of(peer, slot))] if source is None else source,
             dst_ref=held.at[slot, rows_of(t, me), :],
             send_sem=sent,
-            recv_sem=landed.at[slot],
+            recv_sem=landed.at[group_of(slot)],
             device_id={"seq": peer},
             device_id_type=pl.DeviceIdType.MESH,
         )
@@ -119,7 +122,7 @@
         return pltpu.make_async_copy(
             tensors[t].at[:, columns(head_of(me, slot))],
             held.at[slot, rows_of(t, me), :],
-            landed.at[slot],
+            landed.at[group_of(slot)],
         )
 
     def outward(slot, peer):
@@ -217,7 +220,19 @@
     def _(slot):
         @pl.when(has(me, slot))
         def _():
-            wait_bytes(held.at[slot], landed.at[slot])
+            first = has(me, 0) if lead else False
+
+            @pl.when((slot == 0) & first)
+            def _():
+                wait_bytes(held.at[pl.ds(0, early)], landed.at[0])
+
+            @pl.when((slot == lead) & jnp.logical_not(first))
+            def _():
+                wait_bytes(held.at[lead], landed.at[0])
+
+            @pl.when(slot > lead)
+            def _():
+                wait_bytes(held.at[slot], landed.at[group_of(slot)])
 
             @pl.loop(0, total_rows // query_rows)
             def _(block):
@@ -272,9 +287,9 @@
                 def _():
                     outward(slot, peer).start()
 
-    wait_bytes(out_ref, merged)
     for _ in range(3):
         wait_bytes(q_ref, sent)
+    wait_bytes(out_ref, merged)
 
 
 def on_device(queries, key_rows, value_rows):
@@ -298,7 +313,7 @@
             pltpu.VMEM((slots, n, merged_rows, HEAD_DIM), jnp.bfloat16),
             pltpu.VMEM((3, rows, HEAD_DIM), jnp.bfloat16),
             pltpu.SemaphoreType.DMA,
-            pltpu.SemaphoreType.DMA((slots,)),
+            pltpu.SemaphoreType.DMA((heads // n,)),
             pltpu.SemaphoreType.DMA,
             pltpu.SemaphoreType.DMA,
             pltpu.SemaphoreType.REGULAR,

time: 76.9 us -> 76.9 us (level)
  no operation moved by 1% of the time
where the time goes in v4:
time: 76.9 us; the launch traced here: 76.7 us
  Pallas kernels  75.8 us (99%)
  local copies, waits for them, and re-layouts  0.9 us (1%)
    pallas_call x1, Pallas kernels, on_device(): pl.pallas_call(functools.partial(head_kernel, n, heads, math.gcd(total_ro...  75.8 us

profile of v4, /device:TPU:9, one launch (start us, length us, event | category | flops | bytes accessed | tf_op | source)
XLA Modules:
  0.0 76.7 jit_solution(7011516080758762077)
XLA Ops:
  0.0 75.8 %heads_exchange.1 = bf16[256,1664]{1,0:T(8,128)(2,1)S(1)} custom-call(bf16[256,1664]{1,0:T(8,128)(2,1)} %q_ref.1, bf16[256,1664]{1,0:T(8,128)(2,1)} %k_ref.1, bf16[256,1664]{1,0:T(8,128)(2,1)} %v_ref.1), custom_call_target="tpu_custom_call" | custom-call | tf_op jit(solution)/shard_map/heads_exchange/pallas_call | solution.py:305
  75.8 0.9 %copy.5 = bf16[256,1664]{1,0:T(8,128)(2,1)} copy(bf16[256,1664]{1,0:T(8,128)(2,1)S(1)} %heads_exchange.1) | data formatting | bytes 1703936

commit v5 on v4

--- a/solution.py
+++ b/solution.py
@@ -174,16 +174,16 @@
 
     @pl.when(inner)
     def _():
+        @pl.when(jnp.logical_not(left))
+        def _():
+            for t in range(3):
+                inward(t, lead, partner).start()
+
         @pl.when(left)
         def _():
             wait_bytes(staged, loaded)
             for t in range(3):
                 inward(t, lead, partner, staged.at[t]).start()
-
-        @pl.when(jnp.logical_not(left))
-        def _():
-            for t in range(3):
-                inward(t, lead, partner).start()
 
         for slot in range(lead):
             for t in range(3):

time: 76.9 us -> 76.9 us (level)
  no operation moved by 1% of the time
where the time goes in v5:
time: 76.9 us; the launch traced here: 76.7 us
  Pallas kernels  75.8 us (99%)
  local copies, waits for them, and re-layouts  0.9 us (1%)
    pallas_call x1, Pallas kernels, on_device(): pl.pallas_call(functools.partial(head_kernel, n, heads, math.gcd(total_ro...  75.8 us

profile of v5, /device:TPU:9, one launch (start us, length us, event | category | flops | bytes accessed | tf_op | source)
XLA Modules:
  0.0 76.7 jit_solution(11577576852352557677)
XLA Ops:
  0.0 75.8 %heads_exchange.1 = bf16[256,1664]{1,0:T(8,128)(2,1)S(1)} custom-call(bf16[256,1664]{1,0:T(8,128)(2,1)} %q_ref.1, bf16[256,1664]{1,0:T(8,128)(2,1)} %k_ref.1, bf16[256,1664]{1,0:T(8,128)(2,1)} %v_ref.1), custom_call_target="tpu_custom_call" | custom-call | tf_op jit(solution)/shard_map/heads_exchange/pallas_call | solution.py:305
  75.8 0.9 %copy.5 = bf16[256,1664]{1,0:T(8,128)(2,1)} copy(bf16[256,1664]{1,0:T(8,128)(2,1)S(1)} %heads_exchange.1) | data formatting | bytes 1703936

commit v6 on v5

--- a/solution.py
+++ b/solution.py
@@ -72,6 +72,22 @@
     loaded, landed, sent, merged, ready, far,
 ):
     me = lax.axis_index("seq")
+    inner = (me > 0) & (me < n - 1)
+    partner = n - 1 - me
+    mate = me + jnp.where(inner, 1, -1) * jnp.where(me < n // 2, -1, 1)
+
+    def tell(sem, device):
+        pl.semaphore_signal(
+            sem, inc=1, device_id={"seq": device}, device_id_type=pl.DeviceIdType.MESH
+        )
+
+    barrier = pltpu.get_barrier_semaphore()
+
+    @pl.when(inner)
+    def _():
+        tell(barrier, partner)
+        tell(barrier, mate)
+
     flip = lax.rem(lax.axis_index("dp"), 2)
     base, extra = heads // n, heads % n
     lead = 1 if extra else 0
@@ -102,7 +118,8 @@
     def rows_of(tensor, device):
         return pl.ds(pl.multiple_of(tensor * total_rows + device * rows, rows), rows)
 
-    peers = (n - 1 - me, lax.rem(me + n // 2, n), me + 1 - 2 * lax.rem(me, 2))
+    across = me + jnp.where(me < n // 2, n // 2, -(n // 2))
+    peers = (partner, across, mate)
     tensors = (k_ref, q_ref, v_ref)
 
     def group_of(slot):
@@ -143,23 +160,9 @@
     def wait_bytes(ref, sem):
         pltpu.make_async_copy(ref, ref, sem).wait()
 
-    partner, across, mate = peers
     far_low = jnp.where(me < n // 2, n // 2, 0)
     far_high = far_low + 1
-    inner = (me > 0) & (me < n - 1)
     early = lead + 1
-
-    def tell(sem, device):
-        pl.semaphore_signal(
-            sem, inc=1, device_id={"seq": device}, device_id_type=pl.DeviceIdType.MESH
-        )
-
-    barrier = pltpu.get_barrier_semaphore()
-
-    @pl.when(inner)
-    def _():
-        tell(barrier, partner)
-        tell(barrier, mate)
 
     left = me == n // 2 - 1
 

time: 76.9 us -> 76.9 us (level)
  no operation moved by 1% of the time
where the time goes in v6:
time: 76.9 us; the launch traced here: 76.7 us
  Pallas kernels  75.8 us (99%)
  local copies, waits for them, and re-layouts  0.9 us (1%)
    pallas_call x1, Pallas kernels, on_device(): pl.pallas_call(functools.partial(head_kernel, n, heads, math.gcd(total_ro...  75.8 us

profile of v6, /device:TPU:9, one launch (start us, length us, event | category | flops | bytes accessed | tf_op | source)
XLA Modules:
  0.0 76.7 jit_solution(5748785062797130615)
XLA Ops:
  0.0 75.8 %heads_exchange.1 = bf16[256,1664]{1,0:T(8,128)(2,1)S(1)} custom-call(bf16[256,1664]{1,0:T(8,128)(2,1)} %q_ref.1, bf16[256,1664]{1,0:T(8,128)(2,1)} %k_ref.1, bf16[256,1664]{1,0:T(8,128)(2,1)} %v_ref.1), custom_call_target="tpu_custom_call" | custom-call | tf_op jit(solution)/shard_map/heads_exchange/pallas_call | solution.py:308
  75.8 0.9 %copy.5 = bf16[256,1664]{1,0:T(8,128)(2,1)} copy(bf16[256,1664]{1,0:T(8,128)(2,1)S(1)} %heads_exchange.1) | data formatting | bytes 1703936

commit v7 on v6

--- a/solution.py
+++ b/solution.py
@@ -86,6 +86,9 @@
     @pl.when(inner)
     def _():
         tell(barrier, partner)
+
+    @pl.when(me == n // 2 - 1)
+    def _():
         tell(barrier, mate)
 
     flip = lax.rem(lax.axis_index("dp"), 2)
@@ -181,6 +184,7 @@
         def _():
             for t in range(3):
                 inward(t, lead, partner).start()
+            tell(barrier, mate)
 
         @pl.when(left)
         def _():

time: 76.9 us -> 76.9 us (level)
  no operation moved by 1% of the time
where the time goes in v7:
time: 76.9 us; the launch traced here: 76.7 us
  Pallas kernels  75.8 us (99%)
  local copies, waits for them, and re-layouts  0.9 us (1%)
    pallas_call x1, Pallas kernels, on_device(): pl.pallas_call(functools.partial(head_kernel, n, heads, math.gcd(total_ro...  75.8 us

profile of v7, /device:TPU:9, one launch (start us, length us, event | category | flops | bytes accessed | tf_op | source)
XLA Modules:
  0.0 76.7 jit_solution(10670099669592066244)
XLA Ops:
  0.0 75.8 %heads_exchange.1 = bf16[256,1664]{1,0:T(8,128)(2,1)S(1)} custom-call(bf16[256,1664]{1,0:T(8,128)(2,1)} %q_ref.1, bf16[256,1664]{1,0:T(8,128)(2,1)} %k_ref.1, bf16[256,1664]{1,0:T(8,128)(2,1)} %v_ref.1), custom_call_target="tpu_custom_call" | custom-call | tf_op jit(solution)/shard_map/heads_exchange/pallas_call | solution.py:312
  75.8 0.9 %copy.5 = bf16[256,1664]{1,0:T(8,128)(2,1)} copy(bf16[256,1664]{1,0:T(8,128)(2,1)S(1)} %heads_exchange.1) | data formatting | bytes 1703936

commit v8 on v6

--- a/solution.py
+++ b/solution.py
@@ -237,7 +237,7 @@
             def _():
                 wait_bytes(held.at[slot], landed.at[group_of(slot)])
 
-            @pl.loop(0, total_rows // query_rows)
+            @pl.loop(0, total_rows // query_rows, unroll=2)
             def _(block):
                 at = pl.ds(pl.multiple_of(block * query_rows, query_rows), query_rows)
                 from_q = pl.ds(pl.multiple_of(total_rows + block * query_rows, query_rows), query_rows)

time: 76.9 us -> 76.9 us (level)
  no operation moved by 1% of the time
where the time goes in v8:
time: 76.9 us; the launch traced here: 76.8 us
  Pallas kernels  75.9 us (99%)
  local copies, waits for them, and re-layouts  0.9 us (1%)
    pallas_call x1, Pallas kernels, on_device(): pl.pallas_call(functools.partial(head_kernel, n, heads, math.gcd(total_ro...  75.9 us

profile of v8, /device:TPU:9, one launch (start us, length us, event | category | flops | bytes accessed | tf_op | source)
XLA Modules:
  0.0 76.8 jit_solution(896830529132145548)
XLA Ops:
  0.0 75.9 %heads_exchange.1 = bf16[256,1664]{1,0:T(8,128)(2,1)S(1)} custom-call(bf16[256,1664]{1,0:T(8,128)(2,1)} %q_ref.1, bf16[256,1664]{1,0:T(8,128)(2,1)} %k_ref.1, bf16[256,1664]{1,0:T(8,128)(2,1)} %v_ref.1), custom_call_target="tpu_custom_call" | custom-call | tf_op jit(solution)/shard_map/heads_exchange/pallas_call | solution.py:308
  75.9 0.9 %copy.5 = bf16[256,1664]{1,0:T(8,128)(2,1)} copy(bf16[256,1664]{1,0:T(8,128)(2,1)S(1)} %heads_exchange.1) | data formatting | bytes 1703936
